TPU v7x, 512 devices: a whole 4x4x16 slice. The times are simulated.
512 devices in a mesh: gx: 8 (over y_hi, x), gy: 4 (over y_lo, core), gz: 16 (over z).
Axes of the slice: x: 4, y: 4 (y_hi: 2, y_lo: 2; y = y_hi * 2 + y_lo), z: 16, core: 2. Of those that a mesh axis runs over, the one named last changes fastest.
Arguments:
- fields: float32 [6, 128, 64, 2048], P(None, 'gx', 'gy', 'gz'), may hold values from -6 to 6
- permittivity: float32 [128, 64, 2048], P('gx', 'gy', 'gz'), may hold values from 1 to 4
- donor_owner: int32 [65536, 1], P(('gx', 'gy', 'gz')), may hold values from 0 to 63; in each aligned block of 128 rows (0 to 127, 128 to 255, ...) at most 4 rows name the same one
- donor_base: int32 [65536, 3], P(('gx', 'gy', 'gz')), may hold values from 0 to 127, as said below
- donor_weights: float32 [65536, 15], P(('gx', 'gy', 'gz')), may hold values from -3 to 3
Outputs:
- new_fields: float32 [6, 128, 64, 2048], P(None, 'gx', 'gy', 'gz')
- receptor_values: float32 [6, 65536], P(None, ('gx', 'gy', 'gz'))
Inputs may be any that keep to these rules, and one draw needn't show every extreme that they name: `donor_owner`: within the 128 rows of one device no owner index is named by more than 4 rows, and one is named by exactly 4. `donor_base`: column 0 lies in 0 to 15, column 1 in 0 to 15, column 2 in 0 to 127.
All inputs are finite; a program needn't handle non-finite values.
Results may differ from a plain program's by a relative error of at most 0.00002.
Values sent between devices are 32-bit elements; how exact they have to be, the bound alone decides.
No kernel may reach another device: no remote copies, remote signals or barrier semaphores. Data moves between devices by JAX's collectives and lax.ppermute only.
A program may use at most 192 MiB of HBM per device.

v0:
```python
import jax
import jax.numpy as jnp
from jax import lax
from jax.sharding import PartitionSpec as P

step_size = 0.25


def extended(array, sides, width):
    edges = {}
    for axis, dim in sides:
        size, length = (lax.axis_size(axis), array.shape[dim])
        up = [(i, (i + 1) % size) for i in range(size - 1)]
        last = lax.slice_in_dim(array, length - width, length, axis=dim)
        initial = lax.slice_in_dim(array, 0, width, axis=dim)
        edges[dim] = (
            lax.ppermute(last, axis, up),
            lax.ppermute(initial, axis, [(b, a) for a, b in up]),
        )
    done = []
    for _, dim in sides:
        low, high = edges[dim]
        around = [(width, width) if d in done else (0, 0) for d in range(array.ndim)]
        array = jnp.concatenate([jnp.pad(low, around), array, jnp.pad(high, around)], axis=dim)
        done.append(dim)
    return array


def padded_2(cells, sides, width):
    for axis, dim in sides:
        count = lax.axis_size(axis)
        ends = count - 1
        head = lax.slice_in_dim(cells, 0, width, axis=dim)
        tail = lax.slice_in_dim(cells, cells.shape[dim] - width, cells.shape[dim], axis=dim)
        cells = jnp.concatenate(
            [
                lax.ppermute(tail, axis, [(i, (i + 1) % count) for i in range(ends)]),
                cells,
                lax.ppermute(head, axis, [((i + 1) % count, i) for i in range(ends)]),
            ],
            axis=dim,
        )
    return cells


def shifted(field, axis_index, offset):
    window = [slice(2, -2), slice(2, -2), slice(2, -2)]
    length = field.shape[axis_index] - 4
    window[axis_index] = slice(2 + offset, 2 + offset + length)
    return field[tuple(window)]


def derivative(field, axis_index):
    outer = shifted(field, axis_index, -2) - shifted(field, axis_index, 2)
    inner = shifted(field, axis_index, 1) - shifted(field, axis_index, -1)
    return (outer + 8.0 * inner) / 12.0


def curl_rate(padded, coefficient):
    rate_ex = (derivative(padded[5], 1) - derivative(padded[4], 2)) / coefficient
    rate_ey = (derivative(padded[3], 2) - derivative(padded[5], 0)) / coefficient
    rate_ez = (derivative(padded[4], 0) - derivative(padded[3], 1)) / coefficient
    rate_hx = derivative(padded[1], 2) - derivative(padded[2], 1)
    rate_hy = derivative(padded[2], 0) - derivative(padded[0], 2)
    rate_hz = derivative(padded[0], 1) - derivative(padded[1], 0)
    return jnp.stack([rate_ex, rate_ey, rate_ez, rate_hx, rate_hy, rate_hz])


def contract(donor_tiles, weights):
    weight_x = weights[0:5]
    weight_y = weights[5:10]
    weight_z = weights[10:15]
    along_z = jnp.sum(donor_tiles * weight_z[None, None, None, :, :], axis=3)
    along_y = jnp.sum(along_z * weight_y[None, None, :, :], axis=2)
    return jnp.sum(along_y * weight_x[None, :, :], axis=1)


def gather_tiles(donor_grid, corner_rows):
    components, extent_x, extent_y, extent_z = donor_grid.shape
    flat_grid = donor_grid.reshape(components, extent_x * extent_y * extent_z)
    stencil = jnp.arange(5, dtype=jnp.int32)
    offsets = (
        stencil[:, None, None] * (extent_y * extent_z)
        + stencil[None, :, None] * extent_z
        + stencil[None, None, :]
    ).reshape(125)
    starts = corner_rows[0] * (extent_y * extent_z) + corner_rows[1] * extent_z + corner_rows[2]
    picked = jnp.take(flat_grid, offsets[:, None] + starts[None, :], axis=1)
    return picked.reshape(components, 5, 5, 5, corner_rows.shape[1])


def local(fields, permittivity, donor_owner, donor_base, donor_weights):
    accumulated = fields
    taylor_term = fields
    for power in range(1, 5):
        padded = extended(taylor_term, (("gx", 1), ("gy", 2), ("gz", 3)), 2)
        taylor_term = step_size / power * curl_rate(padded, permittivity)
        accumulated = accumulated + taylor_term
    donor_grid = padded_2(accumulated, (("gx", 1), ("gy", 2), ("gz", 3)), 2)
    group_size = lax.axis_size("gy") * lax.axis_size("gz")
    row_count = donor_owner.shape[0]
    capacity = 2 * row_count // group_size
    owner_id = donor_owner[:, 0]
    owner_hits = (owner_id[:, None] == jnp.arange(group_size, dtype=jnp.int32)[None, :]).astype(
        jnp.int32
    )
    earlier = jnp.cumsum(owner_hits, axis=0) - owner_hits
    slot_index = jnp.sum(earlier * owner_hits, axis=1)
    flat_index = owner_id * capacity + slot_index
    corner_send = (
        jnp.zeros((3, group_size * capacity), jnp.int32).at[:, flat_index].set(donor_base.T)
    )
    corner_send = corner_send.reshape(3, group_size, capacity)
    weight_send = (
        jnp.zeros((15, group_size * capacity), jnp.float32).at[:, flat_index].set(donor_weights.T)
    )
    weight_send = weight_send.reshape(15, group_size, capacity)
    donor_corners = lax.all_to_all(
        corner_send, ("gy", "gz"), split_axis=1, concat_axis=1, tiled=True
    )
    piece_weights = lax.all_to_all(
        weight_send, ("gy", "gz"), split_axis=1, concat_axis=1, tiled=True
    )
    slot_count = donor_corners.shape[2]
    donor_tiles = gather_tiles(donor_grid, donor_corners.reshape(3, -1))
    values = contract(donor_tiles, piece_weights.reshape(15, -1)).reshape(6, group_size, slot_count)
    answers = lax.all_to_all(values, ("gy", "gz"), split_axis=1, concat_axis=1, tiled=True)
    receptor_values = answers.reshape(6, -1)[:, flat_index]
    return (accumulated, receptor_values)


def solution(mesh):
    placed = (
        P(None, "gx", "gy", "gz"),
        P("gx", "gy", "gz"),
        P(("gx", "gy", "gz"), None),
        P(("gx", "gy", "gz"), None),
        P(("gx", "gy", "gz"), None),
    )
    return jax.shard_map(
        local,
        mesh=mesh,
        in_specs=placed,
        out_specs=(P(None, "gx", "gy", "gz"), P(None, ("gx", "gy", "gz"))),
        check_vma=False,
    )
```

profile of v0, /device:TPU:14, one launch (start us, length us, event | category | flops | bytes accessed | tf_op | source)
XLA Modules:
  0.0 377.5 jit_solution(17785123580572100083)
XLA Ops:
  3.0 3.8 %collective-permute-start = (f32[6,16,16,2]{2,1,3,0:T(8,128)S(1)}, f32[6,16,16,2]{2,1,3,0:T(8,128)S(1)}, u32[]{:S(2)}, u32[]{:S(2)}) collective-permute-start(f32[6,16,16,2]{2,1,3,0:T(8,128)S(1)} %copy.153), channel_id=1, source_target_pairs={{0,1},{1,2},{2,3},{3,4},{4,5},{5,6},{6,7},{7,8},{8,9},{9,10},{10,1... | collective-permute-start | bytes 36872 | tf_op jit(solution)/shard_map/ppermute | solution.py:17
  10.8 3.6 collective-permute-start.4
  14.5 4.1 %collective-permute-start.2 = (f32[6,2,16,128]{3,2,1,0:T(8,128)S(1)}, f32[6,2,16,128]{3,2,1,0:T(8,128)S(1)}, u32[]{:S(2)}, u32[]{:S(2)}) collective-permute-start(f32[6,2,16,128]{3,2,1,0:T(8,128)S(1)} %get-tuple-element.60), channel_id=1, source_target_pairs={{0,64},{64,128},{128,192},{192,256},{256,320},{320,384},{384,448},... | collective-permute-start | bytes 294920 | tf_op jit(solution)/shard_map/ppermute | solution.py:17
  21.3 19.1 %all-to-all-start = ((s32[3,64,4]{2,0,1:T(4,128)}), s32[3,64,4]{2,0,1:T(4,128)S(1)}, u32[]{:S(2)}, u32[]{:S(2)}) async-start(s32[3,64,4]{2,0,1:T(4,128)} %copy.142), calls=%async_computation | async-start | bytes 262144 | tf_op jit(solution)/shard_map/all_to_all | solution.py:118
  40.4 1.9 collective-permute-start.3
  43.8 7.3 %collective-permute-done.3 = f32[6,2,16,128]{3,2,1,0:T(8,128)S(1)} collective-permute-done((f32[6,2,16,128]{3,2,1,0:T(8,128)S(1)}, f32[6,2,16,128]{3,2,1,0:T(8,128)S(1)}, u32[]{:S(2)}, u32[]{:S(2)}) %collective-permute-start.3) | collective-permute-done | bytes 98336 | tf_op jit(solution)/shard_map/ppermute | solution.py:18
  51.2 2.1 select_maximum_fusion.9
  58.1 2.4 copy.117
  60.5 3.9 %collective-permute-start.6 = (f32[6,16,16,2]{2,1,3,0:T(8,128)}, f32[6,16,16,2]{2,1,3,0:T(8,128)}, u32[]{:S(2)}, u32[]{:S(2)}) collective-permute-start(f32[6,16,16,2]{2,1,3,0:T(8,128)} %copy.117), channel_id=1, source_target_pairs={{0,1},{1,2},{2,3},{3,4},{4,5},{5,6},{6,7},{7,8},{8,9},{9,10},{10,1... | collective-permute-start | bytes 36872 | tf_op jit(solution)/shard_map/ppermute | solution.py:17
  71.7 3.6 collective-permute-start.10
  75.3 1.9 collective-permute-start.8
  77.3 3.9 %collective-permute-start.9 = (f32[6,2,16,128]{3,2,1,0:T(8,128)}, f32[6,2,16,128]{3,2,1,0:T(8,128)}, u32[]{:S(2)}, u32[]{:S(2)}) collective-permute-start(f32[6,2,16,128]{3,2,1,0:T(8,128)} %get-tuple-element.55), channel_id=1, source_target_pairs={{64,0},{128,64},{192,128},{256,192},{320,256},{384,320},{448,384},... | collective-permute-start | bytes 294920 | tf_op jit(solution)/shard_map/ppermute | solution.py:18
  84.9 2.4 copy.166
  89.2 3.1 select_maximum_fusion.6
  96.8 2.4 copy.125
  99.2 5.2 %collective-permute-start.12 = (f32[6,16,16,2]{2,1,3,0:T(8,128)}, f32[6,16,16,2]{2,1,3,0:T(8,128)}, u32[]{:S(2)}, u32[]{:S(2)}) collective-permute-start(f32[6,16,16,2]{2,1,3,0:T(8,128)} %copy.125), channel_id=1, source_target_pairs={{0,1},{1,2},{2,3},{3,4},{4,5},{5,6},{6,7},{7,8},{8,9},{9,10},{10,1... | collective-permute-start | bytes 36872 | tf_op jit(solution)/shard_map/ppermute | solution.py:17
  105.1 2.4 copy.130
  112.8 3.6 collective-permute-start.16
  116.5 5.5 %collective-permute-start.14 = (f32[6,2,16,128]{3,2,1,0:T(8,128)}, f32[6,2,16,128]{3,2,1,0:T(8,128)}, u32[]{:S(2)}, u32[]{:S(2)}) collective-permute-start(f32[6,2,16,128]{3,2,1,0:T(8,128)} %get-tuple-element.48), channel_id=1, source_target_pairs={{0,64},{64,128},{128,192},{192,256},{256,320},{320,384},{384,448},... | collective-permute-start | bytes 294920 | tf_op jit(solution)/shard_map/ppermute | solution.py:17
  122.0 15.8 %all-to-all-start.1 = ((f32[15,64,4]{0,2,1:T(4,128)}), f32[15,64,4]{0,2,1:T(4,128)S(1)}, u32[]{:S(2)}, u32[]{:S(2)}) async-start(f32[15,64,4]{0,2,1:T(4,128)} %bitcast.55), calls=%async_computation.1 | async-start | bytes 262144 | tf_op jit(solution)/shard_map/all_to_all | solution.py:121
  137.9 1.9 collective-permute-start.15
  141.4 2.4 copy.167
  143.8 2.4 copy.170
  148.6 3.2 select_maximum_fusion.3
  157.2 2.4 copy.133
  159.6 4.0 %collective-permute-start.18 = (f32[6,16,16,2]{2,1,3,0:T(8,128)}, f32[6,16,16,2]{2,1,3,0:T(8,128)}, u32[]{:S(2)}, u32[]{:S(2)}) collective-permute-start(f32[6,16,16,2]{2,1,3,0:T(8,128)} %copy.133), channel_id=1, source_target_pairs={{0,1},{1,2},{2,3},{3,4},{4,5},{5,6},{6,7},{7,8},{8,9},{9,10},{10,1... | collective-permute-start | bytes 36872 | tf_op jit(solution)/shard_map/ppermute | solution.py:17
  164.3 2.4 copy.138
  172.1 3.6 collective-permute-start.22
  175.7 7.1 %collective-permute-start.20 = (f32[6,2,16,128]{3,2,1,0:T(8,128)}, f32[6,2,16,128]{3,2,1,0:T(8,128)}, u32[]{:S(2)}, u32[]{:S(2)}) collective-permute-start(f32[6,2,16,128]{3,2,1,0:T(8,128)} %get-tuple-element.42), channel_id=1, source_target_pairs={{0,64},{64,128},{128,192},{192,256},{256,320},{320,384},{384,448},... | collective-permute-start | bytes 294920 | tf_op jit(solution)/shard_map/ppermute | solution.py:17
  182.8 2.1 collective-permute-start.21
  186.6 2.4 copy.171
  189.0 2.4 copy.174
  193.4 3.2 select_maximum_fusion
  199.2 7.5 %collective-permute-start.24 = (f32[6,2,16,128]{3,2,1,0:T(8,128)S(1)}, f32[6,2,16,128]{3,2,1,0:T(8,128)S(1)}, u32[]{:S(2)}, u32[]{:S(2)}) collective-permute-start(f32[6,2,16,128]{3,2,1,0:T(8,128)S(1)} %get-tuple-element.40), channel_id=1, source_target_pairs={{0,64},{64,128},{128,192},{192,256},{256,320},{320,384},{384,448},... | collective-permute-start | bytes 294920 | tf_op jit(solution)/shard_map/ppermute | solution.py:37
  206.8 1.9 collective-permute-start.25
  208.9 7.9 %collective-permute-done.25 = f32[6,2,16,128]{3,2,1,0:T(8,128)S(1)} collective-permute-done((f32[6,2,16,128]{3,2,1,0:T(8,128)S(1)}, f32[6,2,16,128]{3,2,1,0:T(8,128)S(1)}, u32[]{:S(2)}, u32[]{:S(2)}) %collective-permute-start.25) | collective-permute-done | bytes 98336 | tf_op jit(solution)/shard_map/ppermute | solution.py:39
  218.9 3.6 collective-permute-start.27
  226.9 3.0 copy.157
  229.8 5.2 %collective-permute-start.28 = (f32[6,20,20,2]{2,1,3,0:T(8,128)}, f32[6,20,20,2]{2,1,3,0:T(8,128)}, u32[]{:S(2)}, u32[]{:S(2)}) collective-permute-start(f32[6,20,20,2]{2,1,3,0:T(8,128)} %copy.157), channel_id=1, source_target_pairs={{0,1},{1,2},{2,3},{3,4},{4,5},{5,6},{6,7},{7,8},{8,9},{9,10},{10,1... | collective-permute-start | bytes 57608 | tf_op jit(solution)/shard_map/ppermute | solution.py:37
  240.4 3.6 collective-permute-done.29
  244.0 2.9 copy.146
  246.8 4.7 %pad_maximum_fusion = f32[6,20,20,132]{3,2,1,0:T(8,128)} fusion(f32[6,20,20,2]{3,2,1,0:T(8,128)} %copy.146, f32[6,20,2,128]{3,2,1,0:T(2,128)S(1)} %collective-permute-done.27, f32[6,2,16,128]{3,2,1,0:T(8,128)S(1)} %collective-permute-done.25, f32[6,16,16,128]{3,2,1,0:T(8,128)S(1)} %multiply_add_fusion, f32[6,2,16,128]{3,2,1,0:T(8,128)S(1)} %collective-permute-done.24, ...), kind=kLoop, calls=%fused_computation.32 | loop fusion | flops 1900800 | bytes 2534400 | tf_op jit(solution)/shard_map/concatenate | solution.py:35
  251.5 3.3 reshape.199
  254.9 14.0 %copy.147 = f32[6,52800]{0,1:T(8,128)} copy(f32[6,52800]{1,0:T(8,128)S(1)} %reshape.199) | data formatting | bytes 2534400 | tf_op jit(solution)/shard_map/reshape | solution.py:80
  268.8 67.8 %gather_fusion = f32[32000,6]{1,0:T(8,128)} fusion(f32[6,52800]{0,1:T(8,128)} %copy.147, s32[32768]{0:T(1024)S(1)} %pad_clamp_fusion), kind=kCustom, calls=%fused_computation | custom fusion | bytes 1664000 | tf_op jit(solution)/shard_map/jit(_take)/gather | solution.py:88
  336.7 7.9 %multiply_reduce_fusion = f32[6,5,5,256]{0,3,2,1:T(8,128)S(1)} fusion(f32[6,5,5,5,256]{0,4,3,2,1:T(8,128)} %bitcast.166, f32[5,256]{1,0:T(8,128)S(1)} %copy.149, pred[5,5,5,256]{3,2,1,0:T(8,128)(4,1)S(1)} %fusion.10), kind=kLoop, calls=%fused_computation.4 | loop fusion | flops 537600 | bytes 958720 | tf_op jit(solution)/shard_map/reduce_sum | solution.py:73
  345.9 13.9 %all-to-all-start.2 = ((f32[6,64,4]{0,2,1:T(4,128)}), f32[6,64,4]{0,2,1:T(4,128)S(1)}, u32[]{:S(2)}, u32[]{:S(2)}) async-start(f32[6,64,4]{0,2,1:T(4,128)} %bitcast.59), calls=%async_computation.2 | async-start | bytes 262144 | tf_op jit(solution)/shard_map/all_to_all | solution.py:127
  359.8 16.4 %all-to-all-done.2 = f32[6,64,4]{0,2,1:T(4,128)S(1)} async-done(((f32[6,64,4]{0,2,1:T(4,128)}), f32[6,64,4]{0,2,1:T(4,128)S(1)}, u32[]{:S(2)}, u32[]{:S(2)}) %all-to-all-start.2) | async-done | bytes 6176 | tf_op jit(solution)/shard_map/all_to_all | solution.py:127
  (159 shorter events, 74.5 us)
Async XLA Ops:
  0.6 8.2 %copy-start.1 = (f32[6,16,16,128]{3,2,1,0:T(8,128)S(1)}, f32[6,16,16,128]{3,2,1,0:T(8,128)}, u32[]{:S(2)}) copy-start(f32[6,16,16,128]{3,2,1,0:T(8,128)} %param.5) | copy-start | bytes 2359300
  0.6 18.0 %copy-start.8 = (s32[128,1]{0,1:T(1,128)S(1)}, s32[128,1]{0,1:T(1,128)}, u32[]{:S(2)}) copy-start(s32[128,1]{0,1:T(1,128)} %param.7) | copy-start | bytes 1540
  0.6 18.4 %copy-start.9 = (s32[128,3]{0,1:T(4,128)S(1)}, s32[128,3]{0,1:T(4,128)}, u32[]{:S(2)}) copy-start(s32[128,3]{0,1:T(4,128)} %param.8) | copy-start | bytes 4612
  3.0 37.4 %collective-permute-start = (f32[6,16,16,2]{2,1,3,0:T(8,128)S(1)}, f32[6,16,16,2]{2,1,3,0:T(8,128)S(1)}, u32[]{:S(2)}, u32[]{:S(2)}) collective-permute-start(f32[6,16,16,2]{2,1,3,0:T(8,128)S(1)} %copy.153), channel_id=1, source_target_pairs={{0,1},{1,2},{2,3},{3,4},{4,5},{5,6},{6,7},{7,8},{8,9},{9,10},{10,1... | collective-permute-start | bytes 36872 | tf_op jit(solution)/shard_map/ppermute | solution.py:17
  7.5 35.6 %collective-permute-start.5 = (f32[6,16,16,2]{2,1,3,0:T(8,128)S(1)}, f32[6,16,16,2]{2,1,3,0:T(8,128)S(1)}, u32[]{:S(2)}, u32[]{:S(2)}) collective-permute-start(f32[6,16,16,2]{2,1,3,0:T(8,128)S(1)} %copy.156), channel_id=1, source_target_pairs={{1,0},{2,1},{3,2},{4,3},{5,4},{6,5},{7,6},{8,7},{9,8},{10,9},{11,1... | collective-permute-start | bytes 36872 | tf_op jit(solution)/shard_map/ppermute | solution.py:18
  8.9 34.8 %collective-permute-start.1 = (f32[6,16,2,128]{3,1,2,0:T(8,128)S(1)}, f32[6,16,2,128]{3,1,2,0:T(8,128)S(1)}, u32[]{:S(2)}, u32[]{:S(2)}) collective-permute-start(f32[6,16,2,128]{3,1,2,0:T(8,128)S(1)} %copy.154), channel_id=1, source_target_pairs={{0,16},{16,32},{32,48},{1,17},{17,33},{33,49},{2,18},{18,34},{34,5... | collective-permute-start | bytes 294920 | tf_op jit(solution)/shard_map/ppermute | solution.py:17
  10.8 32.9 %collective-permute-start.4 = (f32[6,16,2,128]{3,1,2,0:T(8,128)S(1)}, f32[6,16,2,128]{3,1,2,0:T(8,128)S(1)}, u32[]{:S(2)}, u32[]{:S(2)}) collective-permute-start(f32[6,16,2,128]{3,1,2,0:T(8,128)S(1)} %copy.155), channel_id=1, source_target_pairs={{16,0},{32,16},{48,32},{17,1},{33,17},{49,33},{18,2},{34,18},{50,3... | collective-permute-start | bytes 294920 | tf_op jit(solution)/shard_map/ppermute | solution.py:18
  14.5 29.3 %collective-permute-start.2 = (f32[6,2,16,128]{3,2,1,0:T(8,128)S(1)}, f32[6,2,16,128]{3,2,1,0:T(8,128)S(1)}, u32[]{:S(2)}, u32[]{:S(2)}) collective-permute-start(f32[6,2,16,128]{3,2,1,0:T(8,128)S(1)} %get-tuple-element.60), channel_id=1, source_target_pairs={{0,64},{64,128},{128,192},{192,256},{256,320},{320,384},{384,448},... | collective-permute-start | bytes 294920 | tf_op jit(solution)/shard_map/ppermute | solution.py:17
  21.3 100.8 %all-to-all-start = ((s32[3,64,4]{2,0,1:T(4,128)}), s32[3,64,4]{2,0,1:T(4,128)S(1)}, u32[]{:S(2)}, u32[]{:S(2)}) async-start(s32[3,64,4]{2,0,1:T(4,128)} %copy.142), calls=%async_computation | async-start | bytes 262144 | tf_op jit(solution)/shard_map/all_to_all | solution.py:118
  40.4 10.7 %collective-permute-start.3 = (f32[6,2,16,128]{3,2,1,0:T(8,128)S(1)}, f32[6,2,16,128]{3,2,1,0:T(8,128)S(1)}, u32[]{:S(2)}, u32[]{:S(2)}) collective-permute-start(f32[6,2,16,128]{3,2,1,0:T(8,128)S(1)} %get-tuple-element.61), channel_id=1, source_target_pairs={{64,0},{128,64},{192,128},{256,192},{320,256},{384,320},{448,384},... | collective-permute-start | bytes 294920 | tf_op jit(solution)/shard_map/ppermute | solution.py:18
  53.2 0.9 copy-start
  56.2 25.2 %copy-start.7 = (f32[128,15]{0,1:T(8,128)S(1)}, f32[128,15]{0,1:T(8,128)}, u32[]{:S(2)}) copy-start(f32[128,15]{0,1:T(8,128)} %param.9) | copy-start | bytes 23044
  60.5 16.8 %collective-permute-start.6 = (f32[6,16,16,2]{2,1,3,0:T(8,128)}, f32[6,16,16,2]{2,1,3,0:T(8,128)}, u32[]{:S(2)}, u32[]{:S(2)}) collective-permute-start(f32[6,16,16,2]{2,1,3,0:T(8,128)} %copy.117), channel_id=1, source_target_pairs={{0,1},{1,2},{2,3},{3,4},{4,5},{5,6},{6,7},{7,8},{8,9},{9,10},{10,1... | collective-permute-start | bytes 36872 | tf_op jit(solution)/shard_map/ppermute | solution.py:17
  66.3 18.6 %collective-permute-start.11 = (f32[6,16,16,2]{2,1,3,0:T(8,128)}, f32[6,16,16,2]{2,1,3,0:T(8,128)}, u32[]{:S(2)}, u32[]{:S(2)}) collective-permute-start(f32[6,16,16,2]{2,1,3,0:T(8,128)} %copy.122), channel_id=1, source_target_pairs={{1,0},{2,1},{3,2},{4,3},{5,4},{6,5},{7,6},{8,7},{9,8},{10,9},{11,1... | collective-permute-start | bytes 36872 | tf_op jit(solution)/shard_map/ppermute | solution.py:18
  69.1 18.2 %collective-permute-start.7 = (f32[6,16,2,128]{3,1,2,0:T(8,128)}, f32[6,16,2,128]{3,1,2,0:T(8,128)}, u32[]{:S(2)}, u32[]{:S(2)}) collective-permute-start(f32[6,16,2,128]{3,1,2,0:T(8,128)} %copy.118), channel_id=1, source_target_pairs={{0,16},{16,32},{32,48},{1,17},{17,33},{33,49},{2,18},{18,34},{34,5... | collective-permute-start | bytes 294920 | tf_op jit(solution)/shard_map/ppermute | solution.py:17
  71.7 16.6 %collective-permute-start.10 = (f32[6,16,2,128]{3,1,2,0:T(8,128)}, f32[6,16,2,128]{3,1,2,0:T(8,128)}, u32[]{:S(2)}, u32[]{:S(2)}) collective-permute-start(f32[6,16,2,128]{3,1,2,0:T(8,128)} %copy.119), channel_id=1, source_target_pairs={{16,0},{32,16},{48,32},{17,1},{33,17},{49,33},{18,2},{34,18},{50,3... | collective-permute-start | bytes 294920 | tf_op jit(solution)/shard_map/ppermute | solution.py:18
  75.3 13.9 %collective-permute-start.8 = (f32[6,2,16,128]{3,2,1,0:T(8,128)}, f32[6,2,16,128]{3,2,1,0:T(8,128)}, u32[]{:S(2)}, u32[]{:S(2)}) collective-permute-start(f32[6,2,16,128]{3,2,1,0:T(8,128)} %get-tuple-element.54), channel_id=1, source_target_pairs={{0,64},{64,128},{128,192},{192,256},{256,320},{320,384},{384,448},... | collective-permute-start | bytes 294920 | tf_op jit(solution)/shard_map/ppermute | solution.py:17
  77.3 11.9 %collective-permute-start.9 = (f32[6,2,16,128]{3,2,1,0:T(8,128)}, f32[6,2,16,128]{3,2,1,0:T(8,128)}, u32[]{:S(2)}, u32[]{:S(2)}) collective-permute-start(f32[6,2,16,128]{3,2,1,0:T(8,128)} %get-tuple-element.55), channel_id=1, source_target_pairs={{64,0},{128,64},{192,128},{256,192},{320,256},{384,320},{448,384},... | collective-permute-start | bytes 294920 | tf_op jit(solution)/shard_map/ppermute | solution.py:18
  81.3 0.6 copy-start.5
  99.2 38.7 %collective-permute-start.12 = (f32[6,16,16,2]{2,1,3,0:T(8,128)}, f32[6,16,16,2]{2,1,3,0:T(8,128)}, u32[]{:S(2)}, u32[]{:S(2)}) collective-permute-start(f32[6,16,16,2]{2,1,3,0:T(8,128)} %copy.125), channel_id=1, source_target_pairs={{0,1},{1,2},{2,3},{3,4},{4,5},{5,6},{6,7},{7,8},{8,9},{9,10},{10,1... | collective-permute-start | bytes 36872 | tf_op jit(solution)/shard_map/ppermute | solution.py:17
  107.5 36.4 %collective-permute-start.17 = (f32[6,16,16,2]{2,1,3,0:T(8,128)}, f32[6,16,16,2]{2,1,3,0:T(8,128)}, u32[]{:S(2)}, u32[]{:S(2)}) collective-permute-start(f32[6,16,16,2]{2,1,3,0:T(8,128)} %copy.130), channel_id=1, source_target_pairs={{1,0},{2,1},{3,2},{4,3},{5,4},{6,5},{7,6},{8,7},{9,8},{10,9},{11,1... | collective-permute-start | bytes 36872 | tf_op jit(solution)/shard_map/ppermute | solution.py:18
  110.3 36.0 %collective-permute-start.13 = (f32[6,16,2,128]{3,1,2,0:T(8,128)}, f32[6,16,2,128]{3,1,2,0:T(8,128)}, u32[]{:S(2)}, u32[]{:S(2)}) collective-permute-start(f32[6,16,2,128]{3,1,2,0:T(8,128)} %copy.126), channel_id=1, source_target_pairs={{0,16},{16,32},{32,48},{1,17},{17,33},{33,49},{2,18},{18,34},{34,5... | collective-permute-start | bytes 294920 | tf_op jit(solution)/shard_map/ppermute | solution.py:17
  112.8 34.3 %collective-permute-start.16 = (f32[6,16,2,128]{3,1,2,0:T(8,128)}, f32[6,16,2,128]{3,1,2,0:T(8,128)}, u32[]{:S(2)}, u32[]{:S(2)}) collective-permute-start(f32[6,16,2,128]{3,1,2,0:T(8,128)} %copy.127), channel_id=1, source_target_pairs={{16,0},{32,16},{48,32},{17,1},{33,17},{49,33},{18,2},{34,18},{50,3... | collective-permute-start | bytes 294920 | tf_op jit(solution)/shard_map/ppermute | solution.py:18
  116.5 31.7 %collective-permute-start.14 = (f32[6,2,16,128]{3,2,1,0:T(8,128)}, f32[6,2,16,128]{3,2,1,0:T(8,128)}, u32[]{:S(2)}, u32[]{:S(2)}) collective-permute-start(f32[6,2,16,128]{3,2,1,0:T(8,128)} %get-tuple-element.48), channel_id=1, source_target_pairs={{0,64},{64,128},{128,192},{192,256},{256,320},{320,384},{384,448},... | collective-permute-start | bytes 294920 | tf_op jit(solution)/shard_map/ppermute | solution.py:17
  122.0 116.2 %all-to-all-start.1 = ((f32[15,64,4]{0,2,1:T(4,128)}), f32[15,64,4]{0,2,1:T(4,128)S(1)}, u32[]{:S(2)}, u32[]{:S(2)}) async-start(f32[15,64,4]{0,2,1:T(4,128)} %bitcast.55), calls=%async_computation.1 | async-start | bytes 262144 | tf_op jit(solution)/shard_map/all_to_all | solution.py:121
  137.9 10.7 %collective-permute-start.15 = (f32[6,2,16,128]{3,2,1,0:T(8,128)}, f32[6,2,16,128]{3,2,1,0:T(8,128)}, u32[]{:S(2)}, u32[]{:S(2)}) collective-permute-start(f32[6,2,16,128]{3,2,1,0:T(8,128)} %get-tuple-element.49), channel_id=1, source_target_pairs={{64,0},{128,64},{192,128},{256,192},{320,256},{384,320},{448,384},... | collective-permute-start | bytes 294920 | tf_op jit(solution)/shard_map/ppermute | solution.py:18
  154.1 0.9 copy-start.3
  159.6 23.2 %collective-permute-start.18 = (f32[6,16,16,2]{2,1,3,0:T(8,128)}, f32[6,16,16,2]{2,1,3,0:T(8,128)}, u32[]{:S(2)}, u32[]{:S(2)}) collective-permute-start(f32[6,16,16,2]{2,1,3,0:T(8,128)} %copy.133), channel_id=1, source_target_pairs={{0,1},{1,2},{2,3},{3,4},{4,5},{5,6},{6,7},{7,8},{8,9},{9,10},{10,1... | collective-permute-start | bytes 36872 | tf_op jit(solution)/shard_map/ppermute | solution.py:17
  166.7 22.4 %collective-permute-start.23 = (f32[6,16,16,2]{2,1,3,0:T(8,128)}, f32[6,16,16,2]{2,1,3,0:T(8,128)}, u32[]{:S(2)}, u32[]{:S(2)}) collective-permute-start(f32[6,16,16,2]{2,1,3,0:T(8,128)} %copy.138), channel_id=1, source_target_pairs={{1,0},{2,1},{3,2},{4,3},{5,4},{6,5},{7,6},{8,7},{9,8},{10,9},{11,1... | collective-permute-start | bytes 36872 | tf_op jit(solution)/shard_map/ppermute | solution.py:18
  169.5 21.9 %collective-permute-start.19 = (f32[6,16,2,128]{3,1,2,0:T(8,128)}, f32[6,16,2,128]{3,1,2,0:T(8,128)}, u32[]{:S(2)}, u32[]{:S(2)}) collective-permute-start(f32[6,16,2,128]{3,1,2,0:T(8,128)} %copy.134), channel_id=1, source_target_pairs={{0,16},{16,32},{32,48},{1,17},{17,33},{33,49},{2,18},{18,34},{34,5... | collective-permute-start | bytes 294920 | tf_op jit(solution)/shard_map/ppermute | solution.py:17
  172.1 20.3 %collective-permute-start.22 = (f32[6,16,2,128]{3,1,2,0:T(8,128)}, f32[6,16,2,128]{3,1,2,0:T(8,128)}, u32[]{:S(2)}, u32[]{:S(2)}) collective-permute-start(f32[6,16,2,128]{3,1,2,0:T(8,128)} %copy.135), channel_id=1, source_target_pairs={{16,0},{32,16},{48,32},{17,1},{33,17},{49,33},{18,2},{34,18},{50,3... | collective-permute-start | bytes 294920 | tf_op jit(solution)/shard_map/ppermute | solution.py:18
  175.7 17.6 %collective-permute-start.20 = (f32[6,2,16,128]{3,2,1,0:T(8,128)}, f32[6,2,16,128]{3,2,1,0:T(8,128)}, u32[]{:S(2)}, u32[]{:S(2)}) collective-permute-start(f32[6,2,16,128]{3,2,1,0:T(8,128)} %get-tuple-element.42), channel_id=1, source_target_pairs={{0,64},{64,128},{128,192},{192,256},{256,320},{320,384},{384,448},... | collective-permute-start | bytes 294920 | tf_op jit(solution)/shard_map/ppermute | solution.py:17
  182.8 10.5 %collective-permute-start.21 = (f32[6,2,16,128]{3,2,1,0:T(8,128)}, f32[6,2,16,128]{3,2,1,0:T(8,128)}, u32[]{:S(2)}, u32[]{:S(2)}) collective-permute-start(f32[6,2,16,128]{3,2,1,0:T(8,128)} %get-tuple-element.43), channel_id=1, source_target_pairs={{64,0},{128,64},{192,128},{256,192},{320,256},{384,320},{448,384},... | collective-permute-start | bytes 294920 | tf_op jit(solution)/shard_map/ppermute | solution.py:18
  197.2 1.6 copy-start.4
  198.9 23.7 %copy-start.6 = (s32[5,5,5]{2,1,0:T(8,128)S(1)}, s32[5,5,5]{2,1,0:T(8,128)}, u32[]{:S(2)}) copy-start(s32[5,5,5]{2,1,0:T(8,128)} %copy-done.5) | copy-start | bytes 1504
  199.2 47.7 %copy-start.2 = (f32[6,16,16,128]{3,2,1,0:T(8,128)}, f32[6,16,16,128]{3,2,1,0:T(8,128)S(1)}, u32[]{:S(2)}) copy-start(f32[6,16,16,128]{3,2,1,0:T(8,128)S(1)} %multiply_add_fusion) | copy-start | bytes 2359300
  199.2 9.7 %collective-permute-start.24 = (f32[6,2,16,128]{3,2,1,0:T(8,128)S(1)}, f32[6,2,16,128]{3,2,1,0:T(8,128)S(1)}, u32[]{:S(2)}, u32[]{:S(2)}) collective-permute-start(f32[6,2,16,128]{3,2,1,0:T(8,128)S(1)} %get-tuple-element.40), channel_id=1, source_target_pairs={{0,64},{64,128},{128,192},{192,256},{256,320},{320,384},{384,448},... | collective-permute-start | bytes 294920 | tf_op jit(solution)/shard_map/ppermute | solution.py:37
  206.8 10.1 %collective-permute-start.25 = (f32[6,2,16,128]{3,2,1,0:T(8,128)S(1)}, f32[6,2,16,128]{3,2,1,0:T(8,128)S(1)}, u32[]{:S(2)}, u32[]{:S(2)}) collective-permute-start(f32[6,2,16,128]{3,2,1,0:T(8,128)S(1)} %get-tuple-element.41), channel_id=1, source_target_pairs={{64,0},{128,64},{192,128},{256,192},{320,256},{384,320},{448,384},... | collective-permute-start | bytes 294920 | tf_op jit(solution)/shard_map/ppermute | solution.py:39
  217.0 6.2 %collective-permute-start.26 = (f32[6,20,2,128]{3,2,1,0:T(2,128)S(1)}, f32[6,20,2,128]{3,2,1,0:T(2,128)S(1)}, u32[]{:S(2)}, u32[]{:S(2)}) collective-permute-start(f32[6,20,2,128]{3,2,1,0:T(2,128)S(1)} %get-tuple-element.38), channel_id=1, source_target_pairs={{0,16},{16,32},{32,48},{1,17},{17,33},{33,49},{2,18},{18,34},{34,5... | collective-permute-start | bytes 368648 | tf_op jit(solution)/shard_map/ppermute | solution.py:37
  218.9 6.1 %collective-permute-start.27 = (f32[6,20,2,128]{3,2,1,0:T(2,128)S(1)}, f32[6,20,2,128]{3,2,1,0:T(2,128)S(1)}, u32[]{:S(2)}, u32[]{:S(2)}) collective-permute-start(f32[6,20,2,128]{3,2,1,0:T(2,128)S(1)} %get-tuple-element.39), channel_id=1, source_target_pairs={{16,0},{32,16},{48,32},{17,1},{33,17},{49,33},{18,2},{34,18},{50,3... | collective-permute-start | bytes 368648 | tf_op jit(solution)/shard_map/ppermute | solution.py:39
  229.8 8.8 %collective-permute-start.28 = (f32[6,20,20,2]{2,1,3,0:T(8,128)}, f32[6,20,20,2]{2,1,3,0:T(8,128)}, u32[]{:S(2)}, u32[]{:S(2)}) collective-permute-start(f32[6,20,20,2]{2,1,3,0:T(8,128)} %copy.157), channel_id=1, source_target_pairs={{0,1},{1,2},{2,3},{3,4},{4,5},{5,6},{6,7},{7,8},{8,9},{9,10},{10,1... | collective-permute-start | bytes 57608 | tf_op jit(solution)/shard_map/ppermute | solution.py:37
  236.6 7.3 %collective-permute-start.29 = (f32[6,20,20,2]{2,1,3,0:T(8,128)}, f32[6,20,20,2]{2,1,3,0:T(8,128)}, u32[]{:S(2)}, u32[]{:S(2)}) collective-permute-start(f32[6,20,20,2]{2,1,3,0:T(8,128)} %copy.158), channel_id=1, source_target_pairs={{1,0},{2,1},{3,2},{4,3},{5,4},{6,5},{7,6},{8,7},{9,8},{10,9},{11,1... | collective-permute-start | bytes 57608 | tf_op jit(solution)/shard_map/ppermute | solution.py:39
  345.9 30.3 %all-to-all-start.2 = ((f32[6,64,4]{0,2,1:T(4,128)}), f32[6,64,4]{0,2,1:T(4,128)S(1)}, u32[]{:S(2)}, u32[]{:S(2)}) async-start(f32[6,64,4]{0,2,1:T(4,128)} %bitcast.59), calls=%async_computation.2 | async-start | bytes 262144 | tf_op jit(solution)/shard_map/all_to_all | solution.py:127
where the time goes:
time: 380 us; the launch traced here: 377 us
  local copies, waits for them, and re-layouts  158 us (42%)
  starting transfers between devices  143 us (38%)
  waiting for transfers between devices  38.3 us (10%)
  other arithmetic  36.2 us (10%)
    gather x1, local copies, waits for them, and re-layouts, gather_tiles(): picked = jnp.take(flat_grid, offsets[:, None] + starts[None, :], axis=1)  67.8 us
    ppermute x12, starting transfers between devices, extended(): lax.ppermute(last, axis, up)  43.2 us
    ppermute x12, starting transfers between devices, extended(): lax.ppermute(initial, axis, [(b, a) for a, b in up])  29.6 us
    unnamed x45, local copies, waits for them, and re-layouts  29.2 us
    slice x18, local copies, waits for them, and re-layouts, extended(): last = lax.slice_in_dim(array, length - width, length, axis=dim)  21.8 us
    all_to_all x1, starting transfers between devices, local(): lax.all_to_all(corner_send, ('gy', 'gz'), split_axis=1, concat_axis=1, ti...  19.1 us
    reshape x2, local copies, waits for them, and re-layouts, gather_tiles(): flat_grid = donor_grid.reshape(components, extent_x * extent_y * extent_z)  17.3 us
    all_to_all x1, waiting for transfers between devices, local(): lax.all_to_all(values, ('gy', 'gz'), split_axis=1, concat_axis=1, tiled=T...  16.4 us
  transfers between devices with their start and end apart: 33, of which 8 were waited for; matrix products, arithmetic and copies ran while one was open for 23% of the time, Pallas kernels for 0%

commit v1 on v0

--- a/solution.py
+++ b/solution.py
@@ -115,9 +115,13 @@
         jnp.zeros((15, group_size * capacity), jnp.float32).at[:, flat_index].set(donor_weights.T)
     )
     weight_send = weight_send.reshape(15, group_size, capacity)
-    donor_corners = lax.all_to_all(
-        corner_send, ("gy", "gz"), split_axis=1, concat_axis=1, tiled=True
+    mark_chains = lambda q_in, which_axis: jnp.concatenate(
+        lax.all_to_all(
+            jnp.stack(jnp.split(q_in, lax.axis_size(which_axis), 1), axis=0), which_axis, 0, 0
+        ),
+        1,
     )
+    donor_corners = mark_chains(corner_send, ("gy", "gz"))
     piece_weights = lax.all_to_all(
         weight_send, ("gy", "gz"), split_axis=1, concat_axis=1, tiled=True
     )

time: 380 us -> 384 us (1.011)
  local copies, waits for them, and re-layouts: 158 us -> 163 us
    unnamed x45 -> x109, local copies, waits for them, and re-layouts: 29.2 us -> 35.1 us
  transfers between devices with their start and end apart: 33 -> 33, of which waited for: 8 -> 8; matrix products, arithmetic and copies ran while one was open for 23% -> 24% of each run, Pallas kernels for 0% -> 0%
where the time goes in v1:
time: 384 us; the launch traced here: 382 us
  local copies, waits for them, and re-layouts  163 us (42%)
  starting transfers between devices  142 us (37%)
  waiting for transfers between devices  39.5 us (10%)
  other arithmetic  35.6 us (9%)
    gather x1, local copies, waits for them, and re-layouts, gather_tiles(): picked = jnp.take(flat_grid, offsets[:, None] + starts[None, :], axis=1)  67.9 us
    ppermute x12, starting transfers between devices, extended(): lax.ppermute(last, axis, up)  41.9 us
    unnamed x109, local copies, waits for them, and re-layouts  35.1 us
    ppermute x12, starting transfers between devices, extended(): lax.ppermute(initial, axis, [(b, a) for a, b in up])  29.6 us
    slice x18, local copies, waits for them, and re-layouts, extended(): last = lax.slice_in_dim(array, length - width, length, axis=dim)  21.9 us
    all_to_all x1, starting transfers between devices, local(): lax.all_to_all(jnp.stack(jnp.split(q_in, lax.axis_size(which_axis), 1), a...  19.1 us
    reshape x2, local copies, waits for them, and re-layouts, gather_tiles(): flat_grid = donor_grid.reshape(components, extent_x * extent_y * extent_z)  17.3 us
    all_to_all x1, waiting for transfers between devices, local(): lax.all_to_all(values, ('gy', 'gz'), split_axis=1, concat_axis=1, tiled=T...  16.4 us
  transfers between devices with their start and end apart: 33, of which 8 were waited for; matrix products, arithmetic and copies ran while one was open for 24% of the time, Pallas kernels for 0%

profile of v1, /device:TPU:14, one launch (start us, length us, event | category | flops | bytes accessed | tf_op | source)
XLA Modules:
  0.0 382.1 jit_solution(7020180445564000263)
XLA Ops:
  3.1 3.8 %collective-permute-start = (f32[6,16,16,2]{2,1,3,0:T(8,128)S(1)}, f32[6,16,16,2]{2,1,3,0:T(8,128)S(1)}, u32[]{:S(2)}, u32[]{:S(2)}) collective-permute-start(f32[6,16,16,2]{2,1,3,0:T(8,128)S(1)} %copy.721), channel_id=1, source_target_pairs={{0,1},{1,2},{2,3},{3,4},{4,5},{5,6},{6,7},{7,8},{8,9},{9,10},{10,1... | collective-permute-start | bytes 36872 | tf_op jit(solution)/shard_map/ppermute | solution.py:17
  10.9 3.6 collective-permute-start.4
  14.6 4.1 %collective-permute-start.2 = (f32[6,2,16,128]{3,2,1,0:T(8,128)S(1)}, f32[6,2,16,128]{3,2,1,0:T(8,128)S(1)}, u32[]{:S(2)}, u32[]{:S(2)}) collective-permute-start(f32[6,2,16,128]{3,2,1,0:T(8,128)S(1)} %get-tuple-element.62), channel_id=1, source_target_pairs={{0,64},{64,128},{128,192},{192,256},{256,320},{320,384},{384,448},... | collective-permute-start | bytes 294920 | tf_op jit(solution)/shard_map/ppermute | solution.py:17
  27.2 19.1 %all-to-all-start = ((s32[64,3,1,4]{3,2,1,0:T(1,128)}), s32[64,3,1,4]{3,2,1,0:T(1,128)S(1)}, u32[]{:S(2)}, u32[]{:S(2)}) async-start(s32[64,3,1,4]{3,2,1,0:T(1,128)} %copy.710), calls=%async_computation | async-start | bytes 196608 | tf_op jit(solution)/shard_map/all_to_all | solution.py:119
  46.4 1.9 collective-permute-start.3
  49.8 7.2 %collective-permute-done.3 = f32[6,2,16,128]{3,2,1,0:T(8,128)S(1)} collective-permute-done((f32[6,2,16,128]{3,2,1,0:T(8,128)S(1)}, f32[6,2,16,128]{3,2,1,0:T(8,128)S(1)}, u32[]{:S(2)}, u32[]{:S(2)}) %collective-permute-start.3) | collective-permute-done | bytes 98336 | tf_op jit(solution)/shard_map/ppermute | solution.py:18
  57.0 2.1 select_maximum_fusion.9
  63.9 2.4 copy.621
  66.3 3.9 %collective-permute-start.6 = (f32[6,16,16,2]{2,1,3,0:T(8,128)}, f32[6,16,16,2]{2,1,3,0:T(8,128)}, u32[]{:S(2)}, u32[]{:S(2)}) collective-permute-start(f32[6,16,16,2]{2,1,3,0:T(8,128)} %copy.621), channel_id=1, source_target_pairs={{0,1},{1,2},{2,3},{3,4},{4,5},{5,6},{6,7},{7,8},{8,9},{9,10},{10,1... | collective-permute-start | bytes 36872 | tf_op jit(solution)/shard_map/ppermute | solution.py:17
  77.6 3.6 collective-permute-start.10
  81.2 1.9 collective-permute-start.8
  83.1 3.9 %collective-permute-start.9 = (f32[6,2,16,128]{3,2,1,0:T(8,128)}, f32[6,2,16,128]{3,2,1,0:T(8,128)}, u32[]{:S(2)}, u32[]{:S(2)}) collective-permute-start(f32[6,2,16,128]{3,2,1,0:T(8,128)} %get-tuple-element.57), channel_id=1, source_target_pairs={{64,0},{128,64},{192,128},{256,192},{320,256},{384,320},{448,384},... | collective-permute-start | bytes 294920 | tf_op jit(solution)/shard_map/ppermute | solution.py:18
  90.7 2.4 copy.798
  95.1 3.1 select_maximum_fusion.6
  102.7 2.4 copy.629
  105.1 5.2 %collective-permute-start.12 = (f32[6,16,16,2]{2,1,3,0:T(8,128)}, f32[6,16,16,2]{2,1,3,0:T(8,128)}, u32[]{:S(2)}, u32[]{:S(2)}) collective-permute-start(f32[6,16,16,2]{2,1,3,0:T(8,128)} %copy.629), channel_id=1, source_target_pairs={{0,1},{1,2},{2,3},{3,4},{4,5},{5,6},{6,7},{7,8},{8,9},{9,10},{10,1... | collective-permute-start | bytes 36872 | tf_op jit(solution)/shard_map/ppermute | solution.py:17
  110.9 2.4 copy.634
  118.7 3.6 collective-permute-start.16
  122.3 5.5 %collective-permute-start.14 = (f32[6,2,16,128]{3,2,1,0:T(8,128)}, f32[6,2,16,128]{3,2,1,0:T(8,128)}, u32[]{:S(2)}, u32[]{:S(2)}) collective-permute-start(f32[6,2,16,128]{3,2,1,0:T(8,128)} %get-tuple-element.50), channel_id=1, source_target_pairs={{0,64},{64,128},{128,192},{192,256},{256,320},{320,384},{384,448},... | collective-permute-start | bytes 294920 | tf_op jit(solution)/shard_map/ppermute | solution.py:17
  127.9 15.9 %all-to-all-start.1 = ((f32[15,64,4]{0,2,1:T(4,128)}), f32[15,64,4]{0,2,1:T(4,128)S(1)}, u32[]{:S(2)}, u32[]{:S(2)}) async-start(f32[15,64,4]{0,2,1:T(4,128)} %bitcast.120), calls=%async_computation.1 | async-start | bytes 262144 | tf_op jit(solution)/shard_map/all_to_all | solution.py:125
  143.8 1.9 collective-permute-start.15
  146.0 2.4 copy.799
  148.4 2.4 copy.802
  154.6 3.2 select_maximum_fusion.3
  163.1 2.4 copy.637
  165.5 4.0 %collective-permute-start.18 = (f32[6,16,16,2]{2,1,3,0:T(8,128)}, f32[6,16,16,2]{2,1,3,0:T(8,128)}, u32[]{:S(2)}, u32[]{:S(2)}) collective-permute-start(f32[6,16,16,2]{2,1,3,0:T(8,128)} %copy.637), channel_id=1, source_target_pairs={{0,1},{1,2},{2,3},{3,4},{4,5},{5,6},{6,7},{7,8},{8,9},{9,10},{10,1... | collective-permute-start | bytes 36872 | tf_op jit(solution)/shard_map/ppermute | solution.py:17
  170.2 2.4 copy.642
  178.0 3.6 collective-permute-start.22
  181.7 5.7 %collective-permute-start.20 = (f32[6,2,16,128]{3,2,1,0:T(8,128)}, f32[6,2,16,128]{3,2,1,0:T(8,128)}, u32[]{:S(2)}, u32[]{:S(2)}) collective-permute-start(f32[6,2,16,128]{3,2,1,0:T(8,128)} %get-tuple-element.44), channel_id=1, source_target_pairs={{0,64},{64,128},{128,192},{192,256},{256,320},{320,384},{384,448},... | collective-permute-start | bytes 294920 | tf_op jit(solution)/shard_map/ppermute | solution.py:17
  187.4 2.1 collective-permute-start.21
  191.2 2.4 copy.803
  193.6 2.4 copy.806
  198.0 3.2 select_maximum_fusion
  203.8 7.5 %collective-permute-start.24 = (f32[6,2,16,128]{3,2,1,0:T(8,128)S(1)}, f32[6,2,16,128]{3,2,1,0:T(8,128)S(1)}, u32[]{:S(2)}, u32[]{:S(2)}) collective-permute-start(f32[6,2,16,128]{3,2,1,0:T(8,128)S(1)} %get-tuple-element.42), channel_id=1, source_target_pairs={{0,64},{64,128},{128,192},{192,256},{256,320},{320,384},{384,448},... | collective-permute-start | bytes 294920 | tf_op jit(solution)/shard_map/ppermute | solution.py:37
  213.5 7.9 %collective-permute-done.25 = f32[6,2,16,128]{3,2,1,0:T(8,128)S(1)} collective-permute-done((f32[6,2,16,128]{3,2,1,0:T(8,128)S(1)}, f32[6,2,16,128]{3,2,1,0:T(8,128)S(1)}, u32[]{:S(2)}, u32[]{:S(2)}) %collective-permute-start.25) | collective-permute-done | bytes 98336 | tf_op jit(solution)/shard_map/ppermute | solution.py:39
  221.6 1.9 collective-permute-start.26
  223.5 3.6 collective-permute-start.27
  231.4 3.0 copy.789
  234.4 5.2 %collective-permute-start.28 = (f32[6,20,20,2]{2,1,3,0:T(8,128)}, f32[6,20,20,2]{2,1,3,0:T(8,128)}, u32[]{:S(2)}, u32[]{:S(2)}) collective-permute-start(f32[6,20,20,2]{2,1,3,0:T(8,128)} %copy.789), channel_id=1, source_target_pairs={{0,1},{1,2},{2,3},{3,4},{4,5},{5,6},{6,7},{7,8},{8,9},{9,10},{10,1... | collective-permute-start | bytes 57608 | tf_op jit(solution)/shard_map/ppermute | solution.py:37
  245.0 3.6 collective-permute-done.29
  248.5 2.9 copy.714
  251.4 4.7 %pad_maximum_fusion = f32[6,20,20,132]{3,2,1,0:T(8,128)} fusion(f32[6,20,20,2]{3,2,1,0:T(8,128)} %copy.714, f32[6,20,2,128]{3,2,1,0:T(2,128)S(1)} %collective-permute-done.27, f32[6,2,16,128]{3,2,1,0:T(8,128)S(1)} %collective-permute-done.25, f32[6,16,16,128]{3,2,1,0:T(8,128)S(1)} %multiply_add_fusion, f32[6,2,16,128]{3,2,1,0:T(8,128)S(1)} %collective-permute-done.24, ...), kind=kLoop, calls=%fused_computation.32 | loop fusion | flops 1900800 | bytes 2534400 | tf_op jit(solution)/shard_map/concatenate | solution.py:35
  256.1 3.3 reshape.202
  259.4 14.0 %copy.715 = f32[6,52800]{0,1:T(8,128)} copy(f32[6,52800]{1,0:T(8,128)S(1)} %reshape.202) | data formatting | bytes 2534400 | tf_op jit(solution)/shard_map/reshape | solution.py:80
  273.4 67.9 %gather_fusion = f32[32000,6]{1,0:T(8,128)} fusion(f32[6,52800]{0,1:T(8,128)} %copy.715, s32[32768]{0:T(1024)S(1)} %pad_clamp_fusion), kind=kCustom, calls=%fused_computation | custom fusion | bytes 1664000 | tf_op jit(solution)/shard_map/jit(_take)/gather | solution.py:88
  341.3 7.9 %multiply_reduce_fusion = f32[6,5,5,256]{0,3,2,1:T(8,128)S(1)} fusion(f32[6,5,5,5,256]{0,4,3,2,1:T(8,128)} %bitcast.231, f32[5,256]{1,0:T(8,128)S(1)} %copy.717, pred[5,5,5,256]{3,2,1,0:T(8,128)(4,1)S(1)} %fusion.10), kind=kLoop, calls=%fused_computation.4 | loop fusion | flops 537600 | bytes 958720 | tf_op jit(solution)/shard_map/reduce_sum | solution.py:73
  350.5 13.8 %all-to-all-start.2 = ((f32[6,64,4]{0,2,1:T(4,128)}), f32[6,64,4]{0,2,1:T(4,128)S(1)}, u32[]{:S(2)}, u32[]{:S(2)}) async-start(f32[6,64,4]{0,2,1:T(4,128)} %bitcast.124), calls=%async_computation.2 | async-start | bytes 262144 | tf_op jit(solution)/shard_map/all_to_all | solution.py:131
  364.4 16.4 %all-to-all-done.2 = f32[6,64,4]{0,2,1:T(4,128)S(1)} async-done(((f32[6,64,4]{0,2,1:T(4,128)}), f32[6,64,4]{0,2,1:T(4,128)S(1)}, u32[]{:S(2)}, u32[]{:S(2)}) %all-to-all-start.2) | async-done | bytes 6176 | tf_op jit(solution)/shard_map/all_to_all | solution.py:131
  (228 shorter events, 80.3 us)
Async XLA Ops:
  0.6 8.2 %copy-start.1 = (f32[6,16,16,128]{3,2,1,0:T(8,128)S(1)}, f32[6,16,16,128]{3,2,1,0:T(8,128)}, u32[]{:S(2)}) copy-start(f32[6,16,16,128]{3,2,1,0:T(8,128)} %param.5) | copy-start | bytes 2359300
  0.6 18.1 %copy-start.8 = (s32[128,1]{0,1:T(1,128)S(1)}, s32[128,1]{0,1:T(1,128)}, u32[]{:S(2)}) copy-start(s32[128,1]{0,1:T(1,128)} %param.7) | copy-start | bytes 1540
  0.6 18.5 %copy-start.9 = (s32[128,3]{0,1:T(4,128)S(1)}, s32[128,3]{0,1:T(4,128)}, u32[]{:S(2)}) copy-start(s32[128,3]{0,1:T(4,128)} %param.8) | copy-start | bytes 4612
  3.1 43.3 %collective-permute-start = (f32[6,16,16,2]{2,1,3,0:T(8,128)S(1)}, f32[6,16,16,2]{2,1,3,0:T(8,128)S(1)}, u32[]{:S(2)}, u32[]{:S(2)}) collective-permute-start(f32[6,16,16,2]{2,1,3,0:T(8,128)S(1)} %copy.721), channel_id=1, source_target_pairs={{0,1},{1,2},{2,3},{3,4},{4,5},{5,6},{6,7},{7,8},{8,9},{9,10},{10,1... | collective-permute-start | bytes 36872 | tf_op jit(solution)/shard_map/ppermute | solution.py:17
  7.6 41.5 %collective-permute-start.5 = (f32[6,16,16,2]{2,1,3,0:T(8,128)S(1)}, f32[6,16,16,2]{2,1,3,0:T(8,128)S(1)}, u32[]{:S(2)}, u32[]{:S(2)}) collective-permute-start(f32[6,16,16,2]{2,1,3,0:T(8,128)S(1)} %copy.724), channel_id=1, source_target_pairs={{1,0},{2,1},{3,2},{4,3},{5,4},{6,5},{7,6},{8,7},{9,8},{10,9},{11,1... | collective-permute-start | bytes 36872 | tf_op jit(solution)/shard_map/ppermute | solution.py:18
  9.0 40.7 %collective-permute-start.1 = (f32[6,16,2,128]{3,1,2,0:T(8,128)S(1)}, f32[6,16,2,128]{3,1,2,0:T(8,128)S(1)}, u32[]{:S(2)}, u32[]{:S(2)}) collective-permute-start(f32[6,16,2,128]{3,1,2,0:T(8,128)S(1)} %copy.722), channel_id=1, source_target_pairs={{0,16},{16,32},{32,48},{1,17},{17,33},{33,49},{2,18},{18,34},{34,5... | collective-permute-start | bytes 294920 | tf_op jit(solution)/shard_map/ppermute | solution.py:17
  10.9 38.8 %collective-permute-start.4 = (f32[6,16,2,128]{3,1,2,0:T(8,128)S(1)}, f32[6,16,2,128]{3,1,2,0:T(8,128)S(1)}, u32[]{:S(2)}, u32[]{:S(2)}) collective-permute-start(f32[6,16,2,128]{3,1,2,0:T(8,128)S(1)} %copy.723), channel_id=1, source_target_pairs={{16,0},{32,16},{48,32},{17,1},{33,17},{49,33},{18,2},{34,18},{50,3... | collective-permute-start | bytes 294920 | tf_op jit(solution)/shard_map/ppermute | solution.py:18
  14.6 35.2 %collective-permute-start.2 = (f32[6,2,16,128]{3,2,1,0:T(8,128)S(1)}, f32[6,2,16,128]{3,2,1,0:T(8,128)S(1)}, u32[]{:S(2)}, u32[]{:S(2)}) collective-permute-start(f32[6,2,16,128]{3,2,1,0:T(8,128)S(1)} %get-tuple-element.62), channel_id=1, source_target_pairs={{0,64},{64,128},{128,192},{192,256},{256,320},{320,384},{384,448},... | collective-permute-start | bytes 294920 | tf_op jit(solution)/shard_map/ppermute | solution.py:17
  27.2 100.7 %all-to-all-start = ((s32[64,3,1,4]{3,2,1,0:T(1,128)}), s32[64,3,1,4]{3,2,1,0:T(1,128)S(1)}, u32[]{:S(2)}, u32[]{:S(2)}) async-start(s32[64,3,1,4]{3,2,1,0:T(1,128)} %copy.710), calls=%async_computation | async-start | bytes 196608 | tf_op jit(solution)/shard_map/all_to_all | solution.py:119
  46.4 10.6 %collective-permute-start.3 = (f32[6,2,16,128]{3,2,1,0:T(8,128)S(1)}, f32[6,2,16,128]{3,2,1,0:T(8,128)S(1)}, u32[]{:S(2)}, u32[]{:S(2)}) collective-permute-start(f32[6,2,16,128]{3,2,1,0:T(8,128)S(1)} %get-tuple-element.63), channel_id=1, source_target_pairs={{64,0},{128,64},{192,128},{256,192},{320,256},{384,320},{448,384},... | collective-permute-start | bytes 294920 | tf_op jit(solution)/shard_map/ppermute | solution.py:18
  59.1 0.9 copy-start
  62.0 25.2 %copy-start.7 = (f32[128,15]{0,1:T(8,128)S(1)}, f32[128,15]{0,1:T(8,128)}, u32[]{:S(2)}) copy-start(f32[128,15]{0,1:T(8,128)} %param.9) | copy-start | bytes 23044
  66.3 16.8 %collective-permute-start.6 = (f32[6,16,16,2]{2,1,3,0:T(8,128)}, f32[6,16,16,2]{2,1,3,0:T(8,128)}, u32[]{:S(2)}, u32[]{:S(2)}) collective-permute-start(f32[6,16,16,2]{2,1,3,0:T(8,128)} %copy.621), channel_id=1, source_target_pairs={{0,1},{1,2},{2,3},{3,4},{4,5},{5,6},{6,7},{7,8},{8,9},{9,10},{10,1... | collective-permute-start | bytes 36872 | tf_op jit(solution)/shard_map/ppermute | solution.py:17
  72.2 18.6 %collective-permute-start.11 = (f32[6,16,16,2]{2,1,3,0:T(8,128)}, f32[6,16,16,2]{2,1,3,0:T(8,128)}, u32[]{:S(2)}, u32[]{:S(2)}) collective-permute-start(f32[6,16,16,2]{2,1,3,0:T(8,128)} %copy.626), channel_id=1, source_target_pairs={{1,0},{2,1},{3,2},{4,3},{5,4},{6,5},{7,6},{8,7},{9,8},{10,9},{11,1... | collective-permute-start | bytes 36872 | tf_op jit(solution)/shard_map/ppermute | solution.py:18
  75.0 18.1 %collective-permute-start.7 = (f32[6,16,2,128]{3,1,2,0:T(8,128)}, f32[6,16,2,128]{3,1,2,0:T(8,128)}, u32[]{:S(2)}, u32[]{:S(2)}) collective-permute-start(f32[6,16,2,128]{3,1,2,0:T(8,128)} %copy.622), channel_id=1, source_target_pairs={{0,16},{16,32},{32,48},{1,17},{17,33},{33,49},{2,18},{18,34},{34,5... | collective-permute-start | bytes 294920 | tf_op jit(solution)/shard_map/ppermute | solution.py:17
  77.6 16.5 %collective-permute-start.10 = (f32[6,16,2,128]{3,1,2,0:T(8,128)}, f32[6,16,2,128]{3,1,2,0:T(8,128)}, u32[]{:S(2)}, u32[]{:S(2)}) collective-permute-start(f32[6,16,2,128]{3,1,2,0:T(8,128)} %copy.623), channel_id=1, source_target_pairs={{16,0},{32,16},{48,32},{17,1},{33,17},{49,33},{18,2},{34,18},{50,3... | collective-permute-start | bytes 294920 | tf_op jit(solution)/shard_map/ppermute | solution.py:18
  81.2 13.9 %collective-permute-start.8 = (f32[6,2,16,128]{3,2,1,0:T(8,128)}, f32[6,2,16,128]{3,2,1,0:T(8,128)}, u32[]{:S(2)}, u32[]{:S(2)}) collective-permute-start(f32[6,2,16,128]{3,2,1,0:T(8,128)} %get-tuple-element.56), channel_id=1, source_target_pairs={{0,64},{64,128},{128,192},{192,256},{256,320},{320,384},{384,448},... | collective-permute-start | bytes 294920 | tf_op jit(solution)/shard_map/ppermute | solution.py:17
  83.1 11.9 %collective-permute-start.9 = (f32[6,2,16,128]{3,2,1,0:T(8,128)}, f32[6,2,16,128]{3,2,1,0:T(8,128)}, u32[]{:S(2)}, u32[]{:S(2)}) collective-permute-start(f32[6,2,16,128]{3,2,1,0:T(8,128)} %get-tuple-element.57), channel_id=1, source_target_pairs={{64,0},{128,64},{192,128},{256,192},{320,256},{384,320},{448,384},... | collective-permute-start | bytes 294920 | tf_op jit(solution)/shard_map/ppermute | solution.py:18
  87.1 0.6 copy-start.5
  105.1 38.7 %collective-permute-start.12 = (f32[6,16,16,2]{2,1,3,0:T(8,128)}, f32[6,16,16,2]{2,1,3,0:T(8,128)}, u32[]{:S(2)}, u32[]{:S(2)}) collective-permute-start(f32[6,16,16,2]{2,1,3,0:T(8,128)} %copy.629), channel_id=1, source_target_pairs={{0,1},{1,2},{2,3},{3,4},{4,5},{5,6},{6,7},{7,8},{8,9},{9,10},{10,1... | collective-permute-start | bytes 36872 | tf_op jit(solution)/shard_map/ppermute | solution.py:17
  113.3 35.1 %collective-permute-start.17 = (f32[6,16,16,2]{2,1,3,0:T(8,128)}, f32[6,16,16,2]{2,1,3,0:T(8,128)}, u32[]{:S(2)}, u32[]{:S(2)}) collective-permute-start(f32[6,16,16,2]{2,1,3,0:T(8,128)} %copy.634), channel_id=1, source_target_pairs={{1,0},{2,1},{3,2},{4,3},{5,4},{6,5},{7,6},{8,7},{9,8},{10,9},{11,1... | collective-permute-start | bytes 36872 | tf_op jit(solution)/shard_map/ppermute | solution.py:18
  116.2 34.6 %collective-permute-start.13 = (f32[6,16,2,128]{3,1,2,0:T(8,128)}, f32[6,16,2,128]{3,1,2,0:T(8,128)}, u32[]{:S(2)}, u32[]{:S(2)}) collective-permute-start(f32[6,16,2,128]{3,1,2,0:T(8,128)} %copy.630), channel_id=1, source_target_pairs={{0,16},{16,32},{32,48},{1,17},{17,33},{33,49},{2,18},{18,34},{34,5... | collective-permute-start | bytes 294920 | tf_op jit(solution)/shard_map/ppermute | solution.py:17
  118.7 33.0 %collective-permute-start.16 = (f32[6,16,2,128]{3,1,2,0:T(8,128)}, f32[6,16,2,128]{3,1,2,0:T(8,128)}, u32[]{:S(2)}, u32[]{:S(2)}) collective-permute-start(f32[6,16,2,128]{3,1,2,0:T(8,128)} %copy.631), channel_id=1, source_target_pairs={{16,0},{32,16},{48,32},{17,1},{33,17},{49,33},{18,2},{34,18},{50,3... | collective-permute-start | bytes 294920 | tf_op jit(solution)/shard_map/ppermute | solution.py:18
  122.3 30.4 %collective-permute-start.14 = (f32[6,2,16,128]{3,2,1,0:T(8,128)}, f32[6,2,16,128]{3,2,1,0:T(8,128)}, u32[]{:S(2)}, u32[]{:S(2)}) collective-permute-start(f32[6,2,16,128]{3,2,1,0:T(8,128)} %get-tuple-element.50), channel_id=1, source_target_pairs={{0,64},{64,128},{128,192},{192,256},{256,320},{320,384},{384,448},... | collective-permute-start | bytes 294920 | tf_op jit(solution)/shard_map/ppermute | solution.py:17
  127.9 114.8 %all-to-all-start.1 = ((f32[15,64,4]{0,2,1:T(4,128)}), f32[15,64,4]{0,2,1:T(4,128)S(1)}, u32[]{:S(2)}, u32[]{:S(2)}) async-start(f32[15,64,4]{0,2,1:T(4,128)} %bitcast.120), calls=%async_computation.1 | async-start | bytes 262144 | tf_op jit(solution)/shard_map/all_to_all | solution.py:125
  143.8 10.7 %collective-permute-start.15 = (f32[6,2,16,128]{3,2,1,0:T(8,128)}, f32[6,2,16,128]{3,2,1,0:T(8,128)}, u32[]{:S(2)}, u32[]{:S(2)}) collective-permute-start(f32[6,2,16,128]{3,2,1,0:T(8,128)} %get-tuple-element.51), channel_id=1, source_target_pairs={{64,0},{128,64},{192,128},{256,192},{320,256},{384,320},{448,384},... | collective-permute-start | bytes 294920 | tf_op jit(solution)/shard_map/ppermute | solution.py:18
  160.1 0.9 copy-start.3
  165.5 21.8 %collective-permute-start.18 = (f32[6,16,16,2]{2,1,3,0:T(8,128)}, f32[6,16,16,2]{2,1,3,0:T(8,128)}, u32[]{:S(2)}, u32[]{:S(2)}) collective-permute-start(f32[6,16,16,2]{2,1,3,0:T(8,128)} %copy.637), channel_id=1, source_target_pairs={{0,1},{1,2},{2,3},{3,4},{4,5},{5,6},{6,7},{7,8},{8,9},{9,10},{10,1... | collective-permute-start | bytes 36872 | tf_op jit(solution)/shard_map/ppermute | solution.py:17
  172.6 21.0 %collective-permute-start.23 = (f32[6,16,16,2]{2,1,3,0:T(8,128)}, f32[6,16,16,2]{2,1,3,0:T(8,128)}, u32[]{:S(2)}, u32[]{:S(2)}) collective-permute-start(f32[6,16,16,2]{2,1,3,0:T(8,128)} %copy.642), channel_id=1, source_target_pairs={{1,0},{2,1},{3,2},{4,3},{5,4},{6,5},{7,6},{8,7},{9,8},{10,9},{11,1... | collective-permute-start | bytes 36872 | tf_op jit(solution)/shard_map/ppermute | solution.py:18
  175.5 20.6 %collective-permute-start.19 = (f32[6,16,2,128]{3,1,2,0:T(8,128)}, f32[6,16,2,128]{3,1,2,0:T(8,128)}, u32[]{:S(2)}, u32[]{:S(2)}) collective-permute-start(f32[6,16,2,128]{3,1,2,0:T(8,128)} %copy.638), channel_id=1, source_target_pairs={{0,16},{16,32},{32,48},{1,17},{17,33},{33,49},{2,18},{18,34},{34,5... | collective-permute-start | bytes 294920 | tf_op jit(solution)/shard_map/ppermute | solution.py:17
  178.0 19.0 %collective-permute-start.22 = (f32[6,16,2,128]{3,1,2,0:T(8,128)}, f32[6,16,2,128]{3,1,2,0:T(8,128)}, u32[]{:S(2)}, u32[]{:S(2)}) collective-permute-start(f32[6,16,2,128]{3,1,2,0:T(8,128)} %copy.639), channel_id=1, source_target_pairs={{16,0},{32,16},{48,32},{17,1},{33,17},{49,33},{18,2},{34,18},{50,3... | collective-permute-start | bytes 294920 | tf_op jit(solution)/shard_map/ppermute | solution.py:18
  181.7 16.3 %collective-permute-start.20 = (f32[6,2,16,128]{3,2,1,0:T(8,128)}, f32[6,2,16,128]{3,2,1,0:T(8,128)}, u32[]{:S(2)}, u32[]{:S(2)}) collective-permute-start(f32[6,2,16,128]{3,2,1,0:T(8,128)} %get-tuple-element.44), channel_id=1, source_target_pairs={{0,64},{64,128},{128,192},{192,256},{256,320},{320,384},{384,448},... | collective-permute-start | bytes 294920 | tf_op jit(solution)/shard_map/ppermute | solution.py:17
  187.4 10.6 %collective-permute-start.21 = (f32[6,2,16,128]{3,2,1,0:T(8,128)}, f32[6,2,16,128]{3,2,1,0:T(8,128)}, u32[]{:S(2)}, u32[]{:S(2)}) collective-permute-start(f32[6,2,16,128]{3,2,1,0:T(8,128)} %get-tuple-element.45), channel_id=1, source_target_pairs={{64,0},{128,64},{192,128},{256,192},{320,256},{384,320},{448,384},... | collective-permute-start | bytes 294920 | tf_op jit(solution)/shard_map/ppermute | solution.py:18
  201.8 1.6 copy-start.4
  203.5 23.7 %copy-start.6 = (s32[5,5,5]{2,1,0:T(8,128)S(1)}, s32[5,5,5]{2,1,0:T(8,128)}, u32[]{:S(2)}) copy-start(s32[5,5,5]{2,1,0:T(8,128)} %copy-done.5) | copy-start | bytes 1504
  203.8 47.6 %copy-start.2 = (f32[6,16,16,128]{3,2,1,0:T(8,128)}, f32[6,16,16,128]{3,2,1,0:T(8,128)S(1)}, u32[]{:S(2)}) copy-start(f32[6,16,16,128]{3,2,1,0:T(8,128)S(1)} %multiply_add_fusion) | copy-start | bytes 2359300
  203.8 9.7 %collective-permute-start.24 = (f32[6,2,16,128]{3,2,1,0:T(8,128)S(1)}, f32[6,2,16,128]{3,2,1,0:T(8,128)S(1)}, u32[]{:S(2)}, u32[]{:S(2)}) collective-permute-start(f32[6,2,16,128]{3,2,1,0:T(8,128)S(1)} %get-tuple-element.42), channel_id=1, source_target_pairs={{0,64},{64,128},{128,192},{192,256},{256,320},{320,384},{384,448},... | collective-permute-start | bytes 294920 | tf_op jit(solution)/shard_map/ppermute | solution.py:37
  211.4 10.1 %collective-permute-start.25 = (f32[6,2,16,128]{3,2,1,0:T(8,128)S(1)}, f32[6,2,16,128]{3,2,1,0:T(8,128)S(1)}, u32[]{:S(2)}, u32[]{:S(2)}) collective-permute-start(f32[6,2,16,128]{3,2,1,0:T(8,128)S(1)} %get-tuple-element.43), channel_id=1, source_target_pairs={{64,0},{128,64},{192,128},{256,192},{320,256},{384,320},{448,384},... | collective-permute-start | bytes 294920 | tf_op jit(solution)/shard_map/ppermute | solution.py:39
  221.6 6.2 %collective-permute-start.26 = (f32[6,20,2,128]{3,2,1,0:T(2,128)S(1)}, f32[6,20,2,128]{3,2,1,0:T(2,128)S(1)}, u32[]{:S(2)}, u32[]{:S(2)}) collective-permute-start(f32[6,20,2,128]{3,2,1,0:T(2,128)S(1)} %get-tuple-element.40), channel_id=1, source_target_pairs={{0,16},{16,32},{32,48},{1,17},{17,33},{33,49},{2,18},{18,34},{34,5... | collective-permute-start | bytes 368648 | tf_op jit(solution)/shard_map/ppermute | solution.py:37
  223.5 6.1 %collective-permute-start.27 = (f32[6,20,2,128]{3,2,1,0:T(2,128)S(1)}, f32[6,20,2,128]{3,2,1,0:T(2,128)S(1)}, u32[]{:S(2)}, u32[]{:S(2)}) collective-permute-start(f32[6,20,2,128]{3,2,1,0:T(2,128)S(1)} %get-tuple-element.41), channel_id=1, source_target_pairs={{16,0},{32,16},{48,32},{17,1},{33,17},{49,33},{18,2},{34,18},{50,3... | collective-permute-start | bytes 368648 | tf_op jit(solution)/shard_map/ppermute | solution.py:39
  234.4 8.8 %collective-permute-start.28 = (f32[6,20,20,2]{2,1,3,0:T(8,128)}, f32[6,20,20,2]{2,1,3,0:T(8,128)}, u32[]{:S(2)}, u32[]{:S(2)}) collective-permute-start(f32[6,20,20,2]{2,1,3,0:T(8,128)} %copy.789), channel_id=1, source_target_pairs={{0,1},{1,2},{2,3},{3,4},{4,5},{5,6},{6,7},{7,8},{8,9},{9,10},{10,1... | collective-permute-start | bytes 57608 | tf_op jit(solution)/shard_map/ppermute | solution.py:37
  241.2 7.3 %collective-permute-start.29 = (f32[6,20,20,2]{2,1,3,0:T(8,128)}, f32[6,20,20,2]{2,1,3,0:T(8,128)}, u32[]{:S(2)}, u32[]{:S(2)}) collective-permute-start(f32[6,20,20,2]{2,1,3,0:T(8,128)} %copy.790), channel_id=1, source_target_pairs={{1,0},{2,1},{3,2},{4,3},{5,4},{6,5},{7,6},{8,7},{9,8},{10,9},{11,1... | collective-permute-start | bytes 57608 | tf_op jit(solution)/shard_map/ppermute | solution.py:39
  350.5 30.3 %all-to-all-start.2 = ((f32[6,64,4]{0,2,1:T(4,128)}), f32[6,64,4]{0,2,1:T(4,128)S(1)}, u32[]{:S(2)}, u32[]{:S(2)}) async-start(f32[6,64,4]{0,2,1:T(4,128)} %bitcast.124), calls=%async_computation.2 | async-start | bytes 262144 | tf_op jit(solution)/shard_map/all_to_all | solution.py:131
